TPU v7x, 32 devices: a whole 2x2x4 slice. The times are simulated.
32 devices in a mesh: dp: 4 (over y, x), fsdp: 8 (over z, core).
Axes of the slice: x: 2, y: 2, z: 4, core: 2. Of those that a mesh axis runs over, the one named last changes fastest.
Arguments:
- tokens: bfloat16 [512, 3072], P('dp'), may hold values from -6 to 6
- cotangent: bfloat16 [512, 3072], P('dp'), may hold values from -6 to 6
- routes: int32 [512, 2], P('dp'), may hold values from 0 to 3, all different within a row; in each aligned block of 128 rows (0 to 127, 128 to 255, ...) at most 64 rows name the same one
- router_weight: float32 [512, 2], P('dp'), may hold values from 0.25 to 1
- w_gate: bfloat16 [4, 3072, 8192], P('dp', None, 'fsdp'), may hold values from -0.109375 to 0.109375
- w_up: bfloat16 [4, 3072, 8192], P('dp', None, 'fsdp'), may hold values from -0.109375 to 0.109375
- w_down: bfloat16 [4, 8192, 3072], P('dp', 'fsdp'), may hold values from -0.0625 to 0.0625
Outputs:
- output: bfloat16 [512, 3072], P('dp')
- input_grad: bfloat16 [512, 3072], P('dp')
- grad_gate: bfloat16 [4, 3072, 8192], P('dp', None, 'fsdp')
- grad_up: bfloat16 [4, 3072, 8192], P('dp', None, 'fsdp')
- grad_down: bfloat16 [4, 8192, 3072], P('dp', 'fsdp')
Inputs may be any that keep to these rules, and one draw needn't show every extreme that they name: `routes`: the two experts of a token differ. In the 128 rows of one batch no expert is named by more than 64 rows, a bound that some block reaches in some batches.
All inputs are finite; a program needn't handle non-finite values.
Results may differ from a plain program's by a relative error of at most 0.025.
Values may be sent and summed in bfloat16 or wider, within the bound.
A program may use at most 128 MiB of HBM per device.

v0:
```python
import jax
import jax.numpy as jnp
from jax import lax
from jax.sharding import PartitionSpec as P


def slot_tables(routes, router_weight, experts, capacity):
    expert_ids = jnp.arange(experts, dtype=jnp.int32)
    hit_table = (routes[:, :, None] == expert_ids).astype(jnp.int32)
    per_token = jnp.sum(hit_table, axis=1)
    before = jnp.cumsum(per_token, axis=0) - per_token
    slot_of = jnp.sum(hit_table * before[:, None, :], axis=2)
    slot_ids = jnp.arange(capacity, dtype=jnp.int32)
    placed = hit_table[:, :, :, None] * (slot_of[:, :, None, None] == slot_ids).astype(jnp.int32)
    tok_rows = routes.shape[0]
    flat = placed.reshape(tok_rows, 2, experts * capacity).astype(jnp.float32)
    slot_weight = jnp.sum(flat * router_weight[:, :, None], axis=(0, 1))
    return (flat[:, 0], flat[:, 1], slot_weight)


def on_device(tokens, cotangent, routes, router_weight, w_gate, w_up, w_down):
    experts = lax.axis_size("dp")
    tok_rows, features = tokens.shape
    capacity = max(tok_rows * 3 // 8, tok_rows * 2 // experts, 2)
    local_rows = experts * capacity
    lead = (((0,), (0,)), ((), ()))
    trail = (((1,), (1,)), ((), ()))
    first_pick, second_pick, slot_weight = slot_tables(routes, router_weight, experts, capacity)
    picked = (first_pick + second_pick).astype(jnp.bfloat16)
    send_x = lax.dot_general(picked, tokens, lead, preferred_element_type=jnp.float32).astype(
        jnp.bfloat16
    )
    chosen_dy = lax.dot_general(picked, cotangent, lead, preferred_element_type=jnp.float32)
    send_dy = (chosen_dy * slot_weight[:, None]).astype(jnp.bfloat16)
    arrived_x, arrived_dy = (
        lax.all_to_all(
            send_x.reshape(experts, capacity, features),
            "dp",
            split_axis=0,
            concat_axis=0,
            tiled=True,
        ),
        lax.all_to_all(
            send_dy.reshape(experts, capacity, features),
            "dp",
            split_axis=0,
            concat_axis=0,
            tiled=True,
        ),
    )
    slot_x = arrived_x.reshape(local_rows, features)
    slot_dy = arrived_dy.reshape(local_rows, features)
    gate_w = w_gate[0]
    up_w = w_up[0]
    down_w = w_down[0]
    gate_pre = jnp.dot(slot_x, gate_w, preferred_element_type=jnp.float32)
    up_pre = jnp.dot(slot_x, up_w, preferred_element_type=jnp.float32)
    sigma = jax.nn.sigmoid(gate_pre)
    active = gate_pre * sigma
    hidden = (active * up_pre).astype(jnp.bfloat16)
    out_terms = jnp.dot(hidden, down_w, preferred_element_type=jnp.float32)
    hidden_dy = lax.dot_general(slot_dy, down_w, trail, preferred_element_type=jnp.float32)
    gate_dy = (hidden_dy * up_pre * sigma * (1.0 + gate_pre * (1.0 - sigma))).astype(jnp.bfloat16)
    up_dy = (hidden_dy * active).astype(jnp.bfloat16)
    grad_down = lax.dot_general(hidden, slot_dy, lead, preferred_element_type=jnp.float32).astype(
        jnp.bfloat16
    )
    grad_gate = lax.dot_general(slot_x, gate_dy, lead, preferred_element_type=jnp.float32).astype(
        jnp.bfloat16
    )
    grad_up = lax.dot_general(slot_x, up_dy, lead, preferred_element_type=jnp.float32).astype(
        jnp.bfloat16
    )
    back_terms = lax.dot_general(
        gate_dy, gate_w, trail, preferred_element_type=jnp.float32
    ) + lax.dot_general(up_dy, up_w, trail, preferred_element_type=jnp.float32)
    out_part, back_part = (
        lax.psum_scatter(
            out_terms.reshape(experts, capacity, features).astype(jnp.bfloat16),
            "fsdp",
            scatter_dimension=2,
            tiled=True,
        ).astype(jnp.float32),
        lax.psum_scatter(
            back_terms.reshape(experts, capacity, features).astype(jnp.bfloat16),
            "fsdp",
            scatter_dimension=2,
            tiled=True,
        ).astype(jnp.float32),
    )
    returned_out, returned_dx = (
        lax.all_to_all(
            out_part.astype(jnp.bfloat16), "dp", split_axis=0, concat_axis=0, tiled=True
        ),
        lax.all_to_all(
            back_part.astype(jnp.bfloat16), "dp", split_axis=0, concat_axis=0, tiled=True
        ),
    )
    width = out_part.shape[2]
    flat_out = returned_out.reshape(local_rows, width)
    flat_dx = returned_dx.reshape(local_rows, width)
    first_rows = jnp.dot(
        first_pick.astype(jnp.bfloat16), flat_out, preferred_element_type=jnp.float32
    )
    second_rows = jnp.dot(
        second_pick.astype(jnp.bfloat16), flat_out, preferred_element_type=jnp.float32
    )
    output = (router_weight[:, 0:1] * first_rows + router_weight[:, 1:2] * second_rows).astype(
        jnp.bfloat16
    )
    input_grad = jnp.dot(picked, flat_dx, preferred_element_type=jnp.float32).astype(jnp.bfloat16)
    output, input_grad = (
        lax.all_gather(output, "fsdp", axis=1, tiled=True),
        lax.all_gather(input_grad, "fsdp", axis=1, tiled=True),
    )
    return (output, input_grad, grad_gate[None], grad_up[None], grad_down[None])


def solution(mesh):
    return jax.shard_map(
        on_device,
        mesh=mesh,
        in_specs=(
            P("dp", None),
            P("dp", None),
            P("dp", None),
            P("dp", None),
            P("dp", None, "fsdp"),
            P("dp", None, "fsdp"),
            P("dp", "fsdp", None),
        ),
        out_specs=(
            P("dp", None),
            P("dp", None),
            P("dp", None, "fsdp"),
            P("dp", None, "fsdp"),
            P("dp", "fsdp", None),
        ),
        check_vma=False,
    )
```

profile of v0, /device:TPU:0, one launch (start us, length us, event | category | flops | bytes accessed | tf_op | source)
XLA Modules:
  0.0 201.8 jit_solution(9656438868011355107)
XLA Ops:
  9.8 0.9 multiply_reduce_fusion
  10.7 1.7 fusion.15
  12.5 5.2 %all-to-all-start.2 = ((bf16[4,64,3072]{2,1,0:T(8,128)(2,1)}), bf16[4,64,3072]{2,1,0:T(8,128)(2,1)S(1)}, u32[]{:S(2)}, u32[]{:S(2)}) async-start(bf16[4,64,3072]{2,1,0:T(8,128)(2,1)} %bitcast.89), calls=%async_computation.2 | async-start | bytes 3145728 | tf_op jit(solution)/shard_map/all_to_all | solution.py:43
  17.6 1.7 convolution_convert_fusion
  19.3 17.5 %all-to-all-done.2 = bf16[4,64,3072]{2,1,0:T(8,128)(2,1)S(1)} async-done(((bf16[4,64,3072]{2,1,0:T(8,128)(2,1)}), bf16[4,64,3072]{2,1,0:T(8,128)(2,1)S(1)}, u32[]{:S(2)}, u32[]{:S(2)}) %all-to-all-start.2) | async-done | bytes 1572896 | tf_op jit(solution)/shard_map/all_to_all | solution.py:43
  36.9 3.6 %all-to-all-start = ((bf16[4,64,3072]{2,1,0:T(8,128)(2,1)}), bf16[4,64,3072]{2,1,0:T(8,128)(2,1)S(1)}, u32[]{:S(2)}, u32[]{:S(2)}) async-start(bf16[4,64,3072]{2,1,0:T(8,128)(2,1)} %bitcast.88), calls=%async_computation | async-start | bytes 3145728 | tf_op jit(solution)/shard_map/all_to_all | solution.py:36
  40.5 5.6 %fusion.2 = f32[256,1024]{1,0:T(8,128)} fusion(bf16[256,3072]{1,0:T(8,128)(2,1)S(1)} %bitcast.86, bf16[1,1024,3072]{2,1,0:T(8,128)(2,1)} %param.13), kind=kOutput, calls=%fused_computation.2 | convolution fusion | flops 1610612736 | bytes 8912896 | tf_op jit(solution)/shard_map/dot_general | solution.py:62
  46.1 13.1 %all-to-all-done = bf16[4,64,3072]{2,1,0:T(8,128)(2,1)S(1)} async-done(((bf16[4,64,3072]{2,1,0:T(8,128)(2,1)}), bf16[4,64,3072]{2,1,0:T(8,128)(2,1)S(1)}, u32[]{:S(2)}, u32[]{:S(2)}) %all-to-all-start) | async-done | bytes 1572896 | tf_op jit(solution)/shard_map/all_to_all | solution.py:36
  59.2 4.7 %fusion.6 = f32[256,1024]{1,0:T(8,128)S(1)} fusion(bf16[256,3072]{1,0:T(8,128)(2,1)S(1)} %bitcast.80, bf16[1,3072,1024]{2,1,0:T(8,128)(2,1)} %param.12), kind=kOutput, calls=%fused_computation.6 | convolution fusion | flops 1610612736 | bytes 8912896 | tf_op jit(solution)/shard_map/dot_general | solution.py:57
  64.0 6.2 %multiply_convert_fusion.1 = (bf16[256,1024]{1,0:T(8,128)(2,1)}, bf16[256,1024]{1,0:T(8,128)(2,1)}, bf16[256,1024]{1,0:T(8,128)(2,1)S(1)}) fusion(f32[256,1024]{1,0:T(8,128)S(1)} %copy-done.8, f32[256,1024]{1,0:T(8,128)S(1)} %fusion.6, bf16[256,3072]{1,0:T(8,128)(2,1)S(1)} %bitcast.81, bf16[1,3072,1024]{2,1,0:T(8,128)(2,1)} %param.11), kind=kOutput, calls=%fused_computation.27 | convolution fusion | flops 1614544896 | bytes 11534336 | tf_op jit(solution)/shard_map/dot_general | solution.py:56
  70.9 3.0 %fusion.16 = bf16[4,64,3072]{2,1,0:T(8,128)(2,1)} fusion(bf16[4,64,1024]{2,1,0:T(8,128)(2,1)S(1)} %bitcast.98, bf16[1,1024,3072]{2,1,0:T(8,128)(2,1)S(1)} %bitcast.101), kind=kOutput, calls=%fused_computation.18 | convolution fusion | flops 1611399168 | bytes 8388608 | tf_op jit(solution)/shard_map/dot_general | solution.py:61
  73.9 5.5 %copy.24 = bf16[4,64,3072]{1,0,2:T(4,128)(2,1)} copy(bf16[4,64,3072]{2,1,0:T(8,128)(2,1)} %fusion.16) | data formatting | bytes 3145728
  79.4 5.7 %reshape.77 = bf16[3072,256]{1,0:T(8,128)(2,1)} reshape(bf16[3072,4,64]{2,1,0:T(4,128)(2,1)} %bitcast.84) | data formatting | bytes 3145728
  85.4 4.8 %fusion.4 = f32[256,3072]{1,0:T(8,128)S(1)} fusion(bf16[256,1024]{1,0:T(8,128)(2,1)} %get-tuple-element.6, bf16[1,3072,1024]{2,1,0:T(8,128)(2,1)} %param.12), kind=kOutput, calls=%fused_computation.4 | convolution fusion | flops 1610612736 | bytes 9961472 | tf_op jit(solution)/shard_map/dot_general | solution.py:76
  90.2 6.0 %fusion.19 = bf16[256,3072]{1,0:T(8,128)(2,1)} fusion(f32[256,3072]{1,0:T(8,128)S(1)} %fusion.4, bf16[256,1024]{1,0:T(8,128)(2,1)S(1)} %copy-done.5, bf16[1,3072,1024]{2,1,0:T(8,128)(2,1)} %param.11), kind=kOutput, calls=%fused_computation.19 | convolution fusion | flops 1612185600 | bytes 11534336 | tf_op jit(solution)/shard_map/dot_general | solution.py:74
  96.3 5.5 %copy.26 = bf16[4,64,3072]{1,0,2:T(4,128)(2,1)} copy(bf16[4,64,3072]{2,1,0:T(8,128)(2,1)} %bitcast.97) | data formatting | bytes 3145728
  101.8 5.7 %reshape.79 = bf16[3072,256]{1,0:T(8,128)(2,1)} reshape(bf16[3072,4,64]{2,1,0:T(4,128)(2,1)} %bitcast.85) | data formatting | bytes 3145728
  107.5 5.6 %convert_bitcast_fusion = bf16[1,1024,3072]{2,1,0:T(8,128)(2,1)} fusion(bf16[256,1024]{1,0:T(8,128)(2,1)} %copy-done.2, bf16[256,3072]{1,0:T(8,128)(2,1)S(1)} %bitcast.87), kind=kOutput, calls=%fused_computation.12 | convolution fusion | flops 1613758464 | bytes 8388608 | tf_op jit(solution)/shard_map/dot_general | solution.py:65
  113.2 4.6 %convert_bitcast_fusion.2 = bf16[1,3072,1024]{2,1,0:T(8,128)(2,1)} fusion(bf16[256,3072]{1,0:T(8,128)(2,1)S(1)} %bitcast.82, bf16[256,1024]{1,0:T(8,128)(2,1)S(1)} %copy-done.6), kind=kOutput, calls=%fused_computation.14 | convolution fusion | flops 1613758464 | bytes 8388608 | tf_op jit(solution)/shard_map/dot_general | solution.py:68
  117.8 2.1 %reduce-scatter.7.cloned.1.call-done = bf16[384,256]{1,0:T(8,128)(2,1)} async-done(((bf16[3072,256]{1,0:T(8,128)(2,1)}), bf16[384,256]{1,0:T(8,128)(2,1)}) %reduce-scatter.7.cloned.1.call-update) | async-done | bytes 196624
  119.9 1.2 reshape.78
  121.0 0.9 copy.25
  121.9 3.8 %all-to-all-start.1 = ((bf16[4,64,384]{2,1,0:T(8,128)(2,1)}), bf16[4,64,384]{2,1,0:T(8,128)(2,1)S(1)}, u32[]{:S(2)}, u32[]{:S(2)}) async-start(bf16[4,64,384]{2,1,0:T(8,128)(2,1)} %copy.25), calls=%async_computation.1 | async-start | bytes 393216 | tf_op jit(solution)/shard_map/all_to_all | solution.py:92
  125.8 4.5 %convert_bitcast_fusion.1 = bf16[1,3072,1024]{2,1,0:T(8,128)(2,1)} fusion(bf16[256,3072]{1,0:T(8,128)(2,1)S(1)} %bitcast.83, bf16[256,1024]{1,0:T(8,128)(2,1)S(1)} %copy-done.4), kind=kOutput, calls=%fused_computation.13 | convolution fusion | flops 1613758464 | bytes 8388608 | tf_op jit(solution)/shard_map/dot_general | solution.py:71
  130.3 24.4 %reduce-scatter.9.cloned.1.call-done = bf16[384,256]{1,0:T(8,128)(2,1)} async-done(((bf16[3072,256]{1,0:T(8,128)(2,1)}), bf16[384,256]{1,0:T(8,128)(2,1)}) %reduce-scatter.9.cloned.1.call-update) | async-done | bytes 196624
  154.7 1.2 reshape.80
  155.8 0.9 copy.27
  156.8 3.8 %all-to-all-start.3 = ((bf16[4,64,384]{2,1,0:T(8,128)(2,1)}), bf16[4,64,384]{2,1,0:T(8,128)(2,1)S(1)}, u32[]{:S(2)}, u32[]{:S(2)}) async-start(bf16[4,64,384]{2,1,0:T(8,128)(2,1)} %copy.27), calls=%async_computation.3 | async-start | bytes 393216 | tf_op jit(solution)/shard_map/all_to_all | solution.py:95
  161.0 15.7 %all_gather.6 = bf16[128,3072]{1,0:T(8,128)(2,1)S(1)} all-gather(bf16[128,384]{1,0:T(8,128)(2,1)S(1)} %fusion.23), channel_id=1, replica_groups=mesh['dp'=4,'fsdp'=8] {'fsdp'}, dimensions={1}, use_global_device_ids=true | all-gather | bytes 884736 | tf_op jit(solution)/shard_map/all_gather | solution.py:113
  176.9 16.3 %all_gather.7 = bf16[128,3072]{1,0:T(8,128)(2,1)S(1)} all-gather(bf16[128,384]{1,0:T(8,128)(2,1)S(1)} %convolution_convert_fusion.1), channel_id=1, replica_groups=mesh['dp'=4,'fsdp'=8] {'fsdp'}, dimensions={1}, use_global_device_ids=true | all-gather | bytes 884736 | tf_op jit(solution)/shard_map/all_gather | solution.py:114
  193.2 0.9 copy.30
  194.1 0.9 copy.31
  (44 shorter events, 4.4 us)
Async XLA Ops:
  7.2 3.6 %copy-start = (bf16[128,3072]{1,0:T(8,128)(2,1)S(1)}, bf16[128,3072]{1,0:T(8,128)(2,1)}, u32[]{:S(2)}) copy-start(bf16[128,3072]{1,0:T(8,128)(2,1)} %param.8) | copy-start | bytes 2359300
  9.7 7.9 %copy-start.3 = (bf16[128,3072]{1,0:T(8,128)(2,1)S(1)}, bf16[128,3072]{1,0:T(8,128)(2,1)}, u32[]{:S(2)}) copy-start(bf16[128,3072]{1,0:T(8,128)(2,1)} %param.7) | copy-start | bytes 2359300
  12.5 24.4 %all-to-all-start.2 = ((bf16[4,64,3072]{2,1,0:T(8,128)(2,1)}), bf16[4,64,3072]{2,1,0:T(8,128)(2,1)S(1)}, u32[]{:S(2)}, u32[]{:S(2)}) async-start(bf16[4,64,3072]{2,1,0:T(8,128)(2,1)} %bitcast.89), calls=%async_computation.2 | async-start | bytes 3145728 | tf_op jit(solution)/shard_map/all_to_all | solution.py:43
  36.9 22.3 %all-to-all-start = ((bf16[4,64,3072]{2,1,0:T(8,128)(2,1)}), bf16[4,64,3072]{2,1,0:T(8,128)(2,1)S(1)}, u32[]{:S(2)}, u32[]{:S(2)}) async-start(bf16[4,64,3072]{2,1,0:T(8,128)(2,1)} %bitcast.88), calls=%async_computation | async-start | bytes 3145728 | tf_op jit(solution)/shard_map/all_to_all | solution.py:36
  40.5 79.4 %reduce-scatter.7.cloned.1.call-start = ((), (), s32[]{:S(2)}) async-start(), calls=%async_computation.6 | async-start | bytes 1769472
  59.2 4.7 %copy-start.8 = (f32[256,1024]{1,0:T(8,128)S(1)}, f32[256,1024]{1,0:T(8,128)}, u32[]{:S(2)}) copy-start(f32[256,1024]{1,0:T(8,128)} %fusion.2) | copy-start | bytes 3145732
  59.2 11.7 %slice-start = ((s8[6291456]{0:T(1024)(128)(4,1)}), s8[4194304]{0:T(1024)(128)(4,1)S(1)}, s32[]{:S(2)}) async-start(s8[6291456]{0:T(1024)(128)(4,1)} %bitcast.100), calls=%async_computation.8 | async-start | bytes 8388608
  63.9 7.0 %slice-start.1 = ((s8[6291456]{0:T(1024)(128)(4,1)}), s8[2097152]{0:T(1024)(128)(4,1)S(1)}, s32[]{:S(2)}) async-start(s8[6291456]{0:T(1024)(128)(4,1)} %bitcast.100), calls=%async_computation.9 | async-start | bytes 4194304
  70.1 0.8 copy-start.2
  85.1 69.6 %reduce-scatter.9.cloned.1.call-start = ((), (), s32[]{:S(2)}) async-start(), calls=%async_computation.7 | async-start | bytes 1769472
  85.4 4.9 %copy-start.5 = (bf16[256,1024]{1,0:T(8,128)(2,1)S(1)}, bf16[256,1024]{1,0:T(8,128)(2,1)}, u32[]{:S(2)}) copy-start(bf16[256,1024]{1,0:T(8,128)(2,1)} %get-tuple-element.5) | copy-start | bytes 1572868
  101.8 5.8 %copy-start.7 = (f32[128,2]{0,1:T(2,128)S(1)}, f32[128,2]{0,1:T(2,128)}, u32[]{:S(2)}) copy-start(f32[128,2]{0,1:T(2,128)} %param.10) | copy-start | bytes 3076
  107.5 5.7 %copy-start.6 = (bf16[256,1024]{1,0:T(8,128)(2,1)S(1)}, bf16[256,1024]{1,0:T(8,128)(2,1)}, u32[]{:S(2)}) copy-start(bf16[256,1024]{1,0:T(8,128)(2,1)} %get-tuple-element.5) | copy-start | bytes 1572868
  113.2 12.6 %copy-start.4 = (bf16[256,1024]{1,0:T(8,128)(2,1)S(1)}, bf16[256,1024]{1,0:T(8,128)(2,1)}, u32[]{:S(2)}) copy-start(bf16[256,1024]{1,0:T(8,128)(2,1)} %get-tuple-element.6) | copy-start | bytes 1572868
  121.9 34.8 %all-to-all-start.1 = ((bf16[4,64,384]{2,1,0:T(8,128)(2,1)}), bf16[4,64,384]{2,1,0:T(8,128)(2,1)S(1)}, u32[]{:S(2)}, u32[]{:S(2)}) async-start(bf16[4,64,384]{2,1,0:T(8,128)(2,1)} %copy.25), calls=%async_computation.1 | async-start | bytes 393216 | tf_op jit(solution)/shard_map/all_to_all | solution.py:92
  156.8 19.9 %all-to-all-start.3 = ((bf16[4,64,384]{2,1,0:T(8,128)(2,1)}), bf16[4,64,384]{2,1,0:T(8,128)(2,1)S(1)}, u32[]{:S(2)}, u32[]{:S(2)}) async-start(bf16[4,64,384]{2,1,0:T(8,128)(2,1)} %copy.27), calls=%async_computation.3 | async-start | bytes 393216 | tf_op jit(solution)/shard_map/all_to_all | solution.py:95
  160.5 34.4 %copy-start.1 = (bf16[128,3072]{1,0:T(8,128)(2,1)S(1)}, bf16[128,3072]{1,0:T(8,128)(2,1)}, u32[]{:S(2)}) copy-start(bf16[128,3072]{1,0:T(8,128)(2,1)} %param.8) | copy-start | bytes 2359300
Sparse Core Ops, SparseCore 0:
  85.2 34.5 reduce-scatter.6
  122.2 32.4 reduce-scatter.8
where the time goes:
time: 203 us; the launch traced here: 202 us
  waiting for transfers between devices  57.2 us (28%)
  matrix products  49.1 us (24%)
  blocking collectives  32 us (16%)
  local copies, waits for them, and re-layouts  29.4 us (14%)
  starting transfers between devices  16.6 us (8%)
  between operations  14.2 us (7%)
  other arithmetic  3.26 us (2%)
    unnamed x32, local copies, waits for them, and re-layouts  29.2 us
    unnamed x4, waiting for transfers between devices  26.5 us
    all_to_all x1, waiting for transfers between devices, on_device(): lax.all_to_all(send_dy.reshape(experts, capacity, features), 'dp', split_...  17.5 us
    all_gather x1, blocking collectives, on_device(): lax.all_gather(input_grad, 'fsdp', axis=1, tiled=True)  16.3 us
    all_gather x1, blocking collectives, on_device(): lax.all_gather(output, 'fsdp', axis=1, tiled=True)  15.7 us
    all_to_all x1, waiting for transfers between devices, on_device(): lax.all_to_all(send_x.reshape(experts, capacity, features), 'dp', split_a...  13.1 us
    dot_general x1, matrix products, on_device(): gate_pre = jnp.dot(slot_x, gate_w, preferred_element_type=jnp.float32)  6.17 us
    dot_general x1, matrix products, on_device(): lax.dot_general(gate_dy, gate_w, trail, preferred_element_type=jnp.float32)  6.03 us
  transfers between devices with their start and end apart: 6, of which 4 were waited for; matrix products, arithmetic and copies ran while one was open for 24% of the time, Pallas kernels for 0%

commit v1 on v0

--- a/solution.py
+++ b/solution.py
@@ -1,7 +1,392 @@
+import functools
+
 import jax
 import jax.numpy as jnp
 from jax import lax
+from jax.experimental import pallas as pl
+from jax.experimental.pallas import tpu as pltpu
 from jax.sharding import PartitionSpec as P
+
+MESH = pl.DeviceIdType.MESH
+BF16 = jnp.bfloat16
+F32 = jnp.float32
+LEAD = (((0,), (0,)), ((), ()))
+TRAIL = (((1,), (1,)), ((), ()))
+
+
+def flip(a, mask):
+    bit = 1
+    while bit <= mask:
+        if mask & bit:
+            a = a + bit - 2 * bit * ((a // bit) % 2)
+        bit *= 2
+    return a
+
+
+def mm(a, b, dims=(((1,), (0,)), ((), ()))):
+    return lax.dot_general(a, b, dims, preferred_element_type=F32)
+
+
+def routed_kernel(
+    n, nz, cap, tile,
+    tokens, cotangent, routes_t, rweight_t, rweight, wg_hbm, wu_hbm, wd_hbm,
+    output, input_grad, slots_hbm, hidden_hbm,
+    wg, wu, wd, slots, snd, gpre, upre, hid,
+    core_snd, core_rcv, own, ret_snd, ret, zacc, zsnd, zrcv, fin,
+    w_sem, a_send, a_recv, f_send, f_recv, c_send, c_recv, r_send, r_recv,
+    z_send, z_recv, g_send, g_recv, h_send, h_recv, o_sem,
+):
+    d = lax.axis_index("dp")
+    f = lax.axis_index("fsdp")
+    c = f % 2
+    z = f // 2
+    sib = (d, flip(f, 1))
+    toks, features = tokens.shape
+    half = features // 2
+    rows = n * cap
+    units = hid.shape[2]
+    order = sorted(range(1, n), key=lambda m: -bin(m).count("1"))
+    bits = [1 << s for s in range(nz.bit_length() - 1)]
+
+    def remote(src, dst, ssem, rsem, dev):
+        return pltpu.make_async_remote_copy(
+            src_ref=src, dst_ref=dst, send_sem=ssem, recv_sem=rsem,
+            device_id=dev, device_id_type=MESH,
+        )
+
+    loads = [
+        pltpu.make_async_copy(s, t, w_sem.at[k])
+        for k, (s, t) in enumerate(((wg_hbm, wg), (wu_hbm, wu), (wd_hbm, wd)))
+    ]
+    for load in loads:
+        load.start()
+
+    barrier = pltpu.get_barrier_semaphore()
+    friends = [(flip(d, m), f) for m in order] + [sib] + [(d, flip(f, 2 * b)) for b in bits]
+    for dev in friends:
+        pl.semaphore_signal(barrier, inc=1, device_id=dev, device_id_type=MESH)
+
+    slot_row = lax.broadcasted_iota(jnp.int32, (rows, toks), 0)
+    e_of = slot_row // cap
+    s_of = (slot_row % cap).astype(F32)
+    r = routes_t[...]
+    hit0 = r[0:1, :] == e_of
+    hit1 = r[1:2, :] == e_of
+    per_token = jnp.where(hit0 | hit1, 1.0, 0.0).astype(BF16)
+    earlier = (
+        lax.broadcasted_iota(jnp.int32, (toks, toks), 0)
+        < lax.broadcasted_iota(jnp.int32, (toks, toks), 1)
+    )
+    before = mm(per_token, jnp.where(earlier, 1.0, 0.0).astype(BF16))
+    here = before == s_of
+    first = jnp.where(hit0 & here, 1.0, 0.0)
+    second = jnp.where(hit1 & here, 1.0, 0.0)
+    rw = rweight_t[...]
+    slot_weight = jnp.sum(first * rw[0:1, :] + second * rw[1:2, :], axis=1, keepdims=True)
+    first = first.astype(BF16)
+    second = second.astype(BF16)
+    picked = first + second
+
+    mine = pl.ds(pl.multiple_of(c * half, 128), half)
+    snd[0] = mm(picked, tokens[:, mine]).astype(BF16).reshape(n, cap, half)
+    pl.semaphore_wait(barrier, len(friends))
+
+    sends = []
+
+    def dispatch(t):
+        for m in order:
+            e = flip(d, m)
+            cp = remote(snd.at[t, e], slots.at[c, t, d], a_send.at[t, m], a_recv.at[t, m], (e, f))
+            cp.start()
+            sends.append(cp)
+        slots[c, t, d] = snd[t, d]
+
+    def share(t):
+        for m in [0] + order:
+            b = flip(d, m)
+            if m:
+                remote(
+                    snd.at[t, b], slots.at[c, t, b], a_send.at[t, m], a_recv.at[t, m], (b, f)
+                ).wait_recv()
+            cp = remote(slots.at[c, t, b], slots.at[c, t, b], f_send.at[t, m], f_recv.at[t, m], sib)
+            cp.start()
+            sends.append(cp)
+
+    def shared(t):
+        for m in [0] + order:
+            b = flip(d, m)
+            remote(
+                slots.at[1 - c, t, b], slots.at[1 - c, t, b], f_send.at[t, m], f_recv.at[t, m], sib
+            ).wait_recv()
+
+    dispatch(0)
+    snd[1] = (mm(picked, cotangent[:, mine]) * slot_weight).astype(BF16).reshape(n, cap, half)
+    dispatch(1)
+    share(0)
+    shared(0)
+    loads[0].wait()
+    loads[1].wait()
+
+    def up_step(j, carry):
+        cols = pl.ds(pl.multiple_of(j * tile, tile), tile)
+        x0 = slots[0, 0].reshape(rows, half)
+        x1 = slots[1, 0].reshape(rows, half)
+        g = mm(x0, wg[pl.ds(0, half), cols]) + mm(x1, wg[pl.ds(half, half), cols])
+        u = mm(x0, wu[pl.ds(0, half), cols]) + mm(x1, wu[pl.ds(half, half), cols])
+        gpre[:, cols] = g
+        upre[:, cols] = u
+        hid[0, :, cols] = (g * jax.nn.sigmoid(g) * u).astype(BF16)
+        return carry
+
+    lax.fori_loop(0, units // tile, up_step, 0)
+    loads[2].wait()
+
+    def project(t, term):
+        def theirs(k, carry):
+            cols = pl.ds(pl.multiple_of(k * tile, tile), tile)
+            v = term(pl.ds(pl.multiple_of((1 - c) * half + k * tile, tile), tile))
+            core_snd[t, :, :, cols] = v.astype(BF16).reshape(n, cap, tile)
+            return carry
+
+        def ours(k, carry):
+            cols = pl.ds(pl.multiple_of(k * tile, tile), tile)
+            own[t, :, cols] = term(pl.ds(pl.multiple_of(c * half + k * tile, tile), tile))
+            return carry
+
+        lax.fori_loop(0, half // tile, theirs, 0)
+        cp = remote(core_snd.at[t], core_rcv.at[t], c_send.at[t], c_recv.at[t], sib)
+        cp.start()
+        lax.fori_loop(0, half // tile, ours, 0)
+        cp.wait_recv()
+        sends.append(cp)
+        for m in order + [0]:
+            b = flip(d, m)
+            at = pl.ds(pl.multiple_of(b * cap, 16), cap)
+            v = (own[t, at, :] + core_rcv[t, b].astype(F32)).astype(BF16)
+            if m:
+                ret_snd[t, b] = v
+                cp = remote(ret_snd.at[t, b], ret.at[t, d], r_send.at[t, m], r_recv.at[t, m], (b, f))
+                cp.start()
+                sends.append(cp)
+            else:
+                ret[t, d] = v
+
+    project(0, lambda cols: mm(hid[0], wd[:, cols]))
+
+    share(1)
+    shared(1)
+
+    def down_step(j, carry):
+        cols = pl.ds(pl.multiple_of(j * tile, tile), tile)
+        hdy = mm(slots[0, 1].reshape(rows, half), wd[cols, pl.ds(0, half)], TRAIL) + mm(
+            slots[1, 1].reshape(rows, half), wd[cols, pl.ds(half, half)], TRAIL
+        )
+        g = gpre[:, cols]
+        sig = jax.nn.sigmoid(g)
+        hid[1, :, cols] = (hdy * upre[:, cols] * sig * (1.0 + g * (1.0 - sig))).astype(BF16)
+        hid[2, :, cols] = (hdy * (g * sig)).astype(BF16)
+        return carry
+
+    lax.fori_loop(0, units // tile, down_step, 0)
+    stores = [
+        pltpu.make_async_copy(slots, slots_hbm, o_sem.at[0]),
+        pltpu.make_async_copy(hid, hidden_hbm, o_sem.at[1]),
+    ]
+    for cp in stores:
+        cp.start()
+
+    project(1, lambda cols: mm(hid[1], wg[cols, :], TRAIL) + mm(hid[2], wu[cols, :], TRAIL))
+
+    span = toks // nz
+
+    def combine(t):
+        for m in order:
+            b = flip(d, m)
+            remote(
+                ret_snd.at[t, b], ret.at[t, b], r_send.at[t, m], r_recv.at[t, m], (b, f)
+            ).wait_recv()
+        flat = ret[t].reshape(rows, half)
+        if t == 0:
+            v = rweight[:, 0:1] * mm(first, flat, LEAD) + rweight[:, 1:2] * mm(second, flat, LEAD)
+        else:
+            v = mm(picked, flat, LEAD)
+        zacc[t] = v.reshape(nz, span, half)
+
+    def pieces(s, who):
+        step = bits[s] * 2
+        return [who % step + step * q for q in range(nz // step)]
+
+    base = [sum(nz // (2 * b) for b in bits[:s]) for s in range(len(bits))]
+
+    def reduce_start(t, s):
+        zz = flip(z, bits[s])
+        dev = (d, flip(f, 2 * bits[s]))
+        cps = []
+        for q, p in enumerate(pieces(s, zz)):
+            k = base[s] + q
+            zsnd[t, k] = zacc[t, p].astype(BF16)
+            cp = remote(zsnd.at[t, k], zrcv.at[t, k], z_send.at[t, k], z_recv.at[t, k], dev)
+            cp.start()
+            cps.append(cp)
+        sends.extend(cps)
+        return cps
+
+    def reduce_end(t, s, cps):
+        for q, p in enumerate(pieces(s, z)):
+            cps[q].wait_recv()
+            zacc[t, p] += zrcv[t, base[s] + q].astype(F32)
+
+    def spread_start(t, s):
+        dev = (d, flip(f, 2 * bits[s]))
+        cps = []
+        for q, p in enumerate(pieces(s, z)):
+            k = base[s] + q
+            cp = remote(fin.at[c, t, p], fin.at[c, t, p], g_send.at[t, k], g_recv.at[t, k], dev)
+            cp.start()
+            cps.append(cp)
+        sends.extend(cps)
+        return None
+
+    def spread_end(t, s, cps):
+        dev = (d, flip(f, 2 * bits[s]))
+        for q, p in enumerate(pieces(s, flip(z, bits[s]))):
+            k = base[s] + q
+            remote(
+                fin.at[c, t, p], fin.at[c, t, p], g_send.at[t, k], g_recv.at[t, k], dev
+            ).wait_recv()
+
+    stages = [(reduce_start, reduce_end, s) for s in range(len(bits))]
+    stages += [(spread_start, spread_end, s) for s in reversed(range(len(bits)))]
+
+    def begin(t, i):
+        if i == len(bits):
+            fin[c, t, z] = zacc[t, z].astype(BF16)
+        go, _, s = stages[i]
+        return go(t, s)
+
+    def last(t):
+        cp = remote(fin.at[c, t], fin.at[c, t], h_send.at[t], h_recv.at[t], sib)
+        cp.start()
+        sends.append(cp)
+
+    combine(0)
+    flying = {0: begin(0, 0)}
+    combine(1)
+    flying[1] = begin(1, 0)
+    for i in range(len(stages)):
+        for t in range(2):
+            _, end, s = stages[i]
+            end(t, s, flying[t])
+            if i + 1 < len(stages):
+                flying[t] = begin(t, i + 1)
+            else:
+                last(t)
+
+    for t, result in enumerate((output, input_grad)):
+        remote(
+            fin.at[1 - c, t], fin.at[1 - c, t], h_send.at[t], h_recv.at[t], sib
+        ).wait_recv()
+        for h in range(2):
+            result[:, h * half : (h + 1) * half] = fin[h, t].reshape(toks, half)
+    for cp in sends:
+        cp.wait_send()
+    for cp in stores:
+        cp.wait()
+
+
+def grads_kernel(x, dy, hid, grad_gate, grad_up, grad_down):
+    rows = hid.shape[1]
+    xt = x[0, 0].reshape(rows, x.shape[-1])
+    dyt = dy[0, 0].reshape(rows, dy.shape[-1])
+    grad_gate[...] = mm(xt, hid[1], LEAD).astype(BF16)
+    grad_up[...] = mm(xt, hid[2], LEAD).astype(BF16)
+    grad_down[...] = mm(hid[0], dyt, LEAD).astype(BF16)
+
+
+def fused(tokens, cotangent, routes, router_weight, w_gate, w_up, w_down):
+    n = lax.axis_size("dp")
+    nz = lax.axis_size("fsdp") // 2
+    toks, features = tokens.shape
+    cap = capacity_of(toks, n)
+    rows = n * cap
+    half = features // 2
+    units = w_gate.shape[2]
+    tile = 256
+    span = toks // nz
+    vmem = pl.BlockSpec(memory_space=pltpu.VMEM)
+    hbm = pl.BlockSpec(memory_space=pl.ANY)
+    dma = pltpu.SemaphoreType.DMA
+    V = pltpu.VMEM
+    output, input_grad, slots, hid = pl.pallas_call(
+        functools.partial(routed_kernel, n, nz, cap, tile),
+        out_shape=(
+            jax.ShapeDtypeStruct((toks, features), BF16),
+            jax.ShapeDtypeStruct((toks, features), BF16),
+            jax.ShapeDtypeStruct((2, 2, n, cap, half), BF16),
+            jax.ShapeDtypeStruct((3, rows, units), BF16),
+        ),
+        in_specs=[vmem] * 5 + [hbm] * 3,
+        out_specs=(vmem, vmem, hbm, hbm),
+        scratch_shapes=[
+            V((features, units), BF16),
+            V((features, units), BF16),
+            V((units, features), BF16),
+            V((2, 2, n, cap, half), BF16),
+            V((2, n, cap, half), BF16),
+            V((rows, units), F32),
+            V((rows, units), F32),
+            V((3, rows, units), BF16),
+            V((2, n, cap, half), BF16),
+            V((2, n, cap, half), BF16),
+            V((2, rows, half), F32),
+            V((2, n, cap, half), BF16),
+            V((2, n, cap, half), BF16),
+            V((2, nz, span, half), F32),
+            V((2, nz, span, half), BF16),
+            V((2, nz, span, half), BF16),
+            V((2, 2, nz, span, half), BF16),
+            dma((3,)),
+            dma((2, n)), dma((2, n)), dma((2, n)), dma((2, n)),
+            dma((2,)), dma((2,)),
+            dma((2, n)), dma((2, n)),
+            dma((2, nz)), dma((2, nz)), dma((2, nz)), dma((2, nz)),
+            dma((2,)), dma((2,)),
+            dma((2,)),
+        ],
+        compiler_params=pltpu.CompilerParams(
+            collective_id=0, has_side_effects=True, vmem_limit_bytes=64 * 1000 * 1000
+        ),
+        name="routed",
+    )(tokens, cotangent, routes.T, router_weight.T, router_weight, w_gate[0], w_up[0], w_down[0])
+
+    wide = 512 if half % 512 == 0 else 128
+    per = half // wide
+
+    def slot_spec(t):
+        return pl.BlockSpec((1, 1, n, cap, wide), lambda i: (i // per, t, 0, 0, i % per))
+
+    grad_gate, grad_up, grad_down = pl.pallas_call(
+        grads_kernel,
+        grid=(features // wide,),
+        out_shape=(
+            jax.ShapeDtypeStruct((features, units), BF16),
+            jax.ShapeDtypeStruct((features, units), BF16),
+            jax.ShapeDtypeStruct((units, features), BF16),
+        ),
+        in_specs=[
+            slot_spec(0),
+            slot_spec(1),
+            pl.BlockSpec((3, rows, units), lambda i: (0, 0, 0)),
+        ],
+        out_specs=(
+            pl.BlockSpec((wide, units), lambda i: (i, 0)),
+            pl.BlockSpec((wide, units), lambda i: (i, 0)),
+            pl.BlockSpec((units, wide), lambda i: (0, i)),
+        ),
+        compiler_params=pltpu.CompilerParams(vmem_limit_bytes=60 * 1000 * 1000),
+        name="grads",
+    )(slots, slots, hid)
+    return output, input_grad, grad_gate[None], grad_up[None], grad_down[None]
 
 
 def slot_tables(routes, router_weight, experts, capacity):
@@ -116,9 +501,27 @@
     return (output, input_grad, grad_gate[None], grad_up[None], grad_down[None])
 
 
+def capacity_of(toks, experts):
+    return max(toks * 3 // 8, toks * 2 // experts, 2)
+
+
+def fits(mesh, toks, features, units):
+    n, m = mesh.shape["dp"], mesh.shape["fsdp"]
+    cap = capacity_of(toks, n)
+    powers = n & (n - 1) == 0 and m & (m - 1) == 0 and m >= 4
+    whole = features % 512 == 0 and units % 256 == 0 and cap % 16 == 0 and toks % (8 * m) == 0
+    rows = n * cap
+    held = 6 * features * units + 2 * rows * (13 * features + 7 * units) + 20 * toks * features
+    return powers and whole and held < 56 * 1000 * 1000
+
+
 def solution(mesh):
+    def step(tokens, cotangent, routes, router_weight, w_gate, w_up, w_down):
+        body = fused if fits(mesh, *tokens.shape, w_gate.shape[2]) else on_device
+        return body(tokens, cotangent, routes, router_weight, w_gate, w_up, w_down)
+
     return jax.shard_map(
-        on_device,
+        step,
         mesh=mesh,
         in_specs=(
             P("dp", None),

time: 203 us -> 94.5 us (0.47)
  Pallas kernels: 0 us -> 89.7 us
  waiting for transfers between devices: 57.2 us -> 0 us
  matrix products: 49.1 us -> 0 us
  blocking collectives: 32 us -> 0 us
  local copies, waits for them, and re-layouts: 29.4 us -> 3.18 us
  starting transfers between devices: 16.6 us -> 0 us
  between operations: 14.2 us -> 0.66 us
  other arithmetic: 3.26 us -> 0 us
    pallas_call x0 -> x2, Pallas kernels: none -> 89.7 us  [the longest x1 79.9 us: fused(): pl.pallas_call(functools.partial(routed_kernel, n, nz, cap, tile), out_sh...]
    dot_general x14 -> x0, matrix products: 49.1 us -> none  [the longest x1 6.17 us: on_device(): gate_pre = jnp.dot(slot_x, gate_w, preferred_element_type=jnp.float32)]
    all_gather x2 -> x0, blocking collectives: 32 us -> none  [the longest x1 16.3 us: on_device(): lax.all_gather(input_grad, 'fsdp', axis=1, tiled=True)]
    all_to_all x4 -> x0, waiting for transfers between devices: 30.7 us -> none  [the longest x1 17.5 us: on_device(): lax.all_to_all(send_dy.reshape(experts, capacity, features), 'dp', split_...]
    unnamed x4 -> x0, waiting for transfers between devices: 26.5 us -> none
    unnamed x32 -> x7, local copies, waits for them, and re-layouts: 29.2 us -> 3.18 us
    all_to_all x4 -> x0, starting transfers between devices: 16.3 us -> none  [the longest x1 5.19 us: on_device(): lax.all_to_all(send_dy.reshape(experts, capacity, features), 'dp', split_...]
    reduce_sum x3 -> x0, other arithmetic: 2.35 us -> none  [the longest x1 0.86 us: slot_tables(): slot_weight = jnp.sum(flat * router_weight[:, :, None], axis=(0, 1))]
  transfers between devices with their start and end apart: 6 -> 0, of which waited for: 4 -> 0; matrix products, arithmetic and copies ran while one was open for 24% -> 0% of each run, Pallas kernels for 0% -> 0%
where the time goes in v1:
time: 94.5 us; the launch traced here: 93.5 us
  Pallas kernels  89.7 us (95%)
  local copies, waits for them, and re-layouts  3.18 us (3%)
    pallas_call x1, Pallas kernels, fused(): pl.pallas_call(functools.partial(routed_kernel, n, nz, cap, tile), out_sh...  79.9 us
    pallas_call x1, Pallas kernels, fused(): pl.pallas_call(grads_kernel, grid=(features // wide,), out_shape=(jax.Sha...  9.79 us
    unnamed x7, local copies, waits for them, and re-layouts  3.18 us

profile of v1, /device:TPU:0, one launch (start us, length us, event | category | flops | bytes accessed | tf_op | source)
XLA Modules:
  0.0 93.5 jit_solution(16762455082017323961)
XLA Ops:
  0.6 1.4 %copy.12.rweight = f32[128,2]{1,0:T(8,128)} copy(f32[128,2]{0,1:T(2,128)} %param.10) | data formatting | bytes 2048 | tf_op args[3]
  2.0 79.9 %routed.1 = (bf16[128,3072]{1,0:T(8,128)(2,1)}, bf16[128,3072]{1,0:T(8,128)(2,1)}, bf16[2,2,4,64,1536]{4,3,2,1,0:T(8,128)(2,1)}, bf16[3,256,1024]{2,1,0:T(8,128)(2,1)}) custom-call(bf16[128,3072]{1,0:T(8,128)(2,1)} %tokens.1, bf16[128,3072]{1,0:T(8,128)(2,1)} %cotangent.1, s32[2,128]{1,0:T(2,128)} %bitcast.12, f32[2,128]{1,0:T(2,128)} %bitcast.11, ...), custom_call_target="tpu_custom_call" | custom-call | tf_op jit(solution)/shard_map/routed/pallas_call | solution.py:320
  81.9 0.0 copy-start.1
  81.9 0.0 copy-start
  81.9 9.8 %grads.1 = (bf16[3072,1024]{1,0:T(8,128)(2,1)}, bf16[3072,1024]{1,0:T(8,128)(2,1)}, bf16[1024,3072]{1,0:T(8,128)(2,1)}) custom-call(bf16[2,2,4,64,1536]{4,3,2,1,0:T(8,128)(2,1)} %get-tuple-element.14.x.dy, bf16[2,2,4,64,1536]{4,3,2,1,0:T(8,128)(2,1)} %get-tuple-element.14.x.dy, bf16[3,256,1024]{2,1,0:T(8,128)(2,1)} %get-tuple-element.15.hid), custom_call_target="tpu_custom_call" | custom-call | tf_op jit(solution)/shard_map/grads/pallas_call | solution.py:368
  91.7 0.0 copy-done.1
  91.7 0.9 copy.15
  92.6 0.0 copy-done
  92.6 0.9 copy.16
Async XLA Ops:
  81.9 9.8 %copy-start.1 = (bf16[128,3072]{1,0:T(8,128)(2,1)S(1)}, bf16[128,3072]{1,0:T(8,128)(2,1)}, u32[]{:S(2)}) copy-start(bf16[128,3072]{1,0:T(8,128)(2,1)} %get-tuple-element.24) | copy-start | bytes 2359300
  81.9 10.7 %copy-start = (bf16[128,3072]{1,0:T(8,128)(2,1)S(1)}, bf16[128,3072]{1,0:T(8,128)(2,1)}, u32[]{:S(2)}) copy-start(bf16[128,3072]{1,0:T(8,128)(2,1)} %get-tuple-element.25) | copy-start | bytes 2359300

commit v2 on v1

--- a/solution.py
+++ b/solution.py
@@ -28,7 +28,7 @@
 
 
 def routed_kernel(
-    n, nz, cap, tile,
+    n, nz, cap, tile, chunks, lag,
     tokens, cotangent, routes_t, rweight_t, rweight, wg_hbm, wu_hbm, wd_hbm,
     output, input_grad, slots_hbm, hidden_hbm,
     wg, wu, wd, slots, snd, gpre, upre, hid,
@@ -43,6 +43,7 @@
     sib = (d, flip(f, 1))
     toks, features = tokens.shape
     half = features // 2
+    width = half // chunks
     rows = n * cap
     units = hid.shape[2]
     order = sorted(range(1, n), key=lambda m: -bin(m).count("1"))
@@ -142,34 +143,51 @@
     loads[2].wait()
 
     def project(t, term):
-        def theirs(k, carry):
+        def theirs(q, k, carry):
             cols = pl.ds(pl.multiple_of(k * tile, tile), tile)
-            v = term(pl.ds(pl.multiple_of((1 - c) * half + k * tile, tile), tile))
-            core_snd[t, :, :, cols] = v.astype(BF16).reshape(n, cap, tile)
+            at = pl.multiple_of((1 - c) * half + q * width + k * tile, tile)
+            v = term(pl.ds(at, tile))
+            core_snd[t, q, :, :, cols] = v.astype(BF16).reshape(n, cap, tile)
             return carry
 
-        def ours(k, carry):
+        def ours(q, k, carry):
             cols = pl.ds(pl.multiple_of(k * tile, tile), tile)
-            own[t, :, cols] = term(pl.ds(pl.multiple_of(c * half + k * tile, tile), tile))
+            at = pl.multiple_of(c * half + q * width + k * tile, tile)
+            own[t, q, :, cols] = term(pl.ds(at, tile))
             return carry
 
-        lax.fori_loop(0, half // tile, theirs, 0)
-        cp = remote(core_snd.at[t], core_rcv.at[t], c_send.at[t], c_recv.at[t], sib)
-        cp.start()
-        lax.fori_loop(0, half // tile, ours, 0)
-        cp.wait_recv()
-        sends.append(cp)
-        for m in order + [0]:
-            b = flip(d, m)
-            at = pl.ds(pl.multiple_of(b * cap, 16), cap)
-            v = (own[t, at, :] + core_rcv[t, b].astype(F32)).astype(BF16)
-            if m:
-                ret_snd[t, b] = v
-                cp = remote(ret_snd.at[t, b], ret.at[t, d], r_send.at[t, m], r_recv.at[t, m], (b, f))
-                cp.start()
-                sends.append(cp)
-            else:
-                ret[t, d] = v
+        halves = []
+        for q in range(chunks):
+            lax.fori_loop(0, width // tile, functools.partial(theirs, q), 0)
+            cp = remote(
+                core_snd.at[t, q], core_rcv.at[t, q], c_send.at[t, q], c_recv.at[t, q], sib
+            )
+            cp.start()
+            halves.append(cp)
+        for q in range(chunks):
+            lax.fori_loop(0, width // tile, functools.partial(ours, q), 0)
+            halves[q].wait_recv()
+            for m in order + [0]:
+                b = flip(d, m)
+                at = pl.ds(pl.multiple_of(b * cap, 16), cap)
+                v = (own[t, q, at, :] + core_rcv[t, q, b].astype(F32)).astype(BF16)
+                if m:
+                    ret_snd[t, q, b] = v
+                    cp = returned(t, q, m, b, d)
+                    cp.start()
+                    sends.append(cp)
+                else:
+                    ret[t, q, d] = v
+        sends.extend(halves)
+
+    def returned(t, q, m, b, where):
+        return remote(
+            ret_snd.at[t, q, b],
+            ret.at[t, q, where],
+            r_send.at[t, q, m],
+            r_recv.at[t, q, m],
+            (b, f),
+        )
 
     project(0, lambda cols: mm(hid[0], wd[:, cols]))
 
@@ -199,18 +217,16 @@
 
     span = toks // nz
 
-    def combine(t):
+    def combine(t, q):
         for m in order:
             b = flip(d, m)
-            remote(
-                ret_snd.at[t, b], ret.at[t, b], r_send.at[t, m], r_recv.at[t, m], (b, f)
-            ).wait_recv()
-        flat = ret[t].reshape(rows, half)
+            returned(t, q, m, b, b).wait_recv()
+        flat = ret[t, q].reshape(rows, width)
         if t == 0:
             v = rweight[:, 0:1] * mm(first, flat, LEAD) + rweight[:, 1:2] * mm(second, flat, LEAD)
         else:
             v = mm(picked, flat, LEAD)
-        zacc[t] = v.reshape(nz, span, half)
+        zacc[t, q] = v.reshape(nz, span, width)
 
     def pieces(s, who):
         step = bits[s] * 2
@@ -218,76 +234,76 @@
 
     base = [sum(nz // (2 * b) for b in bits[:s]) for s in range(len(bits))]
 
-    def reduce_start(t, s):
-        zz = flip(z, bits[s])
+    def summing(t, q, s, k):
         dev = (d, flip(f, 2 * bits[s]))
-        cps = []
-        for q, p in enumerate(pieces(s, zz)):
-            k = base[s] + q
-            zsnd[t, k] = zacc[t, p].astype(BF16)
-            cp = remote(zsnd.at[t, k], zrcv.at[t, k], z_send.at[t, k], z_recv.at[t, k], dev)
+        return remote(
+            zsnd.at[t, q, k], zrcv.at[t, q, k], z_send.at[t, q, k], z_recv.at[t, q, k], dev
+        )
+
+    def spreading(t, q, s, k, p):
+        dev = (d, flip(f, 2 * bits[s]))
+        piece = fin.at[c, t, q, p]
+        return remote(piece, piece, g_send.at[t, q, k], g_recv.at[t, q, k], dev)
+
+    def reduce_start(t, q, s):
+        for i, p in enumerate(pieces(s, flip(z, bits[s]))):
+            k = base[s] + i
+            zsnd[t, q, k] = zacc[t, q, p].astype(BF16)
+            cp = summing(t, q, s, k)
             cp.start()
-            cps.append(cp)
-        sends.extend(cps)
-        return cps
-
-    def reduce_end(t, s, cps):
-        for q, p in enumerate(pieces(s, z)):
-            cps[q].wait_recv()
-            zacc[t, p] += zrcv[t, base[s] + q].astype(F32)
-
-    def spread_start(t, s):
-        dev = (d, flip(f, 2 * bits[s]))
-        cps = []
-        for q, p in enumerate(pieces(s, z)):
-            k = base[s] + q
-            cp = remote(fin.at[c, t, p], fin.at[c, t, p], g_send.at[t, k], g_recv.at[t, k], dev)
+            sends.append(cp)
+
+    def reduce_end(t, q, s):
+        for i, p in enumerate(pieces(s, z)):
+            k = base[s] + i
+            summing(t, q, s, k).wait_recv()
+            zacc[t, q, p] += zrcv[t, q, k].astype(F32)
+
+    def spread_start(t, q, s):
+        for i, p in enumerate(pieces(s, z)):
+            cp = spreading(t, q, s, base[s] + i, p)
             cp.start()
-            cps.append(cp)
-        sends.extend(cps)
-        return None
-
-    def spread_end(t, s, cps):
-        dev = (d, flip(f, 2 * bits[s]))
-        for q, p in enumerate(pieces(s, flip(z, bits[s]))):
-            k = base[s] + q
-            remote(
-                fin.at[c, t, p], fin.at[c, t, p], g_send.at[t, k], g_recv.at[t, k], dev
-            ).wait_recv()
+            sends.append(cp)
+
+    def spread_end(t, q, s):
+        for i, p in enumerate(pieces(s, flip(z, bits[s]))):
+            spreading(t, q, s, base[s] + i, p).wait_recv()
+
+    def last(t, q, h):
+        piece = fin.at[h, t, q]
+        return remote(piece, piece, h_send.at[t, q], h_recv.at[t, q], sib)
 
     stages = [(reduce_start, reduce_end, s) for s in range(len(bits))]
     stages += [(spread_start, spread_end, s) for s in reversed(range(len(bits)))]
 
-    def begin(t, i):
+    def advance(t, q, i):
+        if i == 0:
+            combine(t, q)
+        else:
+            _, end, s = stages[i - 1]
+            end(t, q, s)
         if i == len(bits):
-            fin[c, t, z] = zacc[t, z].astype(BF16)
-        go, _, s = stages[i]
-        return go(t, s)
-
-    def last(t):
-        cp = remote(fin.at[c, t], fin.at[c, t], h_send.at[t], h_recv.at[t], sib)
-        cp.start()
-        sends.append(cp)
-
-    combine(0)
-    flying = {0: begin(0, 0)}
-    combine(1)
-    flying[1] = begin(1, 0)
-    for i in range(len(stages)):
-        for t in range(2):
-            _, end, s = stages[i]
-            end(t, s, flying[t])
-            if i + 1 < len(stages):
-                flying[t] = begin(t, i + 1)
-            else:
-                last(t)
+            fin[c, t, q, z] = zacc[t, q, z].astype(BF16)
+        if i < len(stages):
+            begin, _, s = stages[i]
+            begin(t, q, s)
+        else:
+            cp = last(t, q, c)
+            cp.start()
+            sends.append(cp)
+
+    todo = [
+        (i + lag * t, t, q, i) for i in range(len(stages) + 1) for t in range(2) for q in range(chunks)
+    ]
+    for _, t, q, i in sorted(todo):
+        advance(t, q, i)
 
     for t, result in enumerate((output, input_grad)):
-        remote(
-            fin.at[1 - c, t], fin.at[1 - c, t], h_send.at[t], h_recv.at[t], sib
-        ).wait_recv()
-        for h in range(2):
-            result[:, h * half : (h + 1) * half] = fin[h, t].reshape(toks, half)
+        for q in range(chunks):
+            last(t, q, 1 - c).wait_recv()
+            for h in range(2):
+                at = h * half + q * width
+                result[:, at : at + width] = fin[h, t, q].reshape(toks, width)
     for cp in sends:
         cp.wait_send()
     for cp in stores:
@@ -312,13 +328,15 @@
     half = features // 2
     units = w_gate.shape[2]
     tile = 256
+    chunks = 2
+    width = half // chunks
     span = toks // nz
     vmem = pl.BlockSpec(memory_space=pltpu.VMEM)
     hbm = pl.BlockSpec(memory_space=pl.ANY)
     dma = pltpu.SemaphoreType.DMA
     V = pltpu.VMEM
     output, input_grad, slots, hid = pl.pallas_call(
-        functools.partial(routed_kernel, n, nz, cap, tile),
+        functools.partial(routed_kernel, n, nz, cap, tile, chunks, 2),
         out_shape=(
             jax.ShapeDtypeStruct((toks, features), BF16),
             jax.ShapeDtypeStruct((toks, features), BF16),
@@ -336,21 +354,21 @@
             V((rows, units), F32),
             V((rows, units), F32),
             V((3, rows, units), BF16),
-            V((2, n, cap, half), BF16),
-            V((2, n, cap, half), BF16),
-            V((2, rows, half), F32),
-            V((2, n, cap, half), BF16),
-            V((2, n, cap, half), BF16),
-            V((2, nz, span, half), F32),
-            V((2, nz, span, half), BF16),
-            V((2, nz, span, half), BF16),
-            V((2, 2, nz, span, half), BF16),
+            V((2, chunks, n, cap, width), BF16),
+            V((2, chunks, n, cap, width), BF16),
+            V((2, chunks, rows, width), F32),
+            V((2, chunks, n, cap, width), BF16),
+            V((2, chunks, n, cap, width), BF16),
+            V((2, chunks, nz, span, width), F32),
+            V((2, chunks, nz, span, width), BF16),
+            V((2, chunks, nz, span, width), BF16),
+            V((2, 2, chunks, nz, span, width), BF16),
             dma((3,)),
             dma((2, n)), dma((2, n)), dma((2, n)), dma((2, n)),
-            dma((2,)), dma((2,)),
-            dma((2, n)), dma((2, n)),
-            dma((2, nz)), dma((2, nz)), dma((2, nz)), dma((2, nz)),
-            dma((2,)), dma((2,)),
+            dma((2, chunks)), dma((2, chunks)),
+            dma((2, chunks, n)), dma((2, chunks, n)),
+            dma((2, chunks, nz)), dma((2, chunks, nz)), dma((2, chunks, nz)), dma((2, chunks, nz)),
+            dma((2, chunks)), dma((2, chunks)),
             dma((2,)),
         ],
         compiler_params=pltpu.CompilerParams(
@@ -509,7 +527,7 @@
     n, m = mesh.shape["dp"], mesh.shape["fsdp"]
     cap = capacity_of(toks, n)
     powers = n & (n - 1) == 0 and m & (m - 1) == 0 and m >= 4
-    whole = features % 512 == 0 and units % 256 == 0 and cap % 16 == 0 and toks % (8 * m) == 0
+    whole = features % 1024 == 0 and units % 256 == 0 and cap % 16 == 0 and toks % (8 * m) == 0
     rows = n * cap
     held = 6 * features * units + 2 * rows * (13 * features + 7 * units) + 20 * toks * features
     return powers and whole and held < 56 * 1000 * 1000

time: 94.5 us -> 89.8 us (0.950)
  Pallas kernels: 89.7 us -> 85.6 us
    pallas_call x1, Pallas kernels: 79.9 us -> 75.8 us  [fused(): pl.pallas_call(functools.partial(routed_kernel, n, nz, cap, tile, chunks,...]
where the time goes in v2:
time: 89.8 us; the launch traced here: 89.5 us
  Pallas kernels  85.6 us (95%)
  local copies, waits for them, and re-layouts  3.18 us (4%)
    pallas_call x1, Pallas kernels, fused(): pl.pallas_call(functools.partial(routed_kernel, n, nz, cap, tile, chunks,...  75.8 us
    pallas_call x1, Pallas kernels, fused(): pl.pallas_call(grads_kernel, grid=(features // wide,), out_shape=(jax.Sha...  9.79 us
    unnamed x7, local copies, waits for them, and re-layouts  3.18 us

profile of v2, /device:TPU:0, one launch (start us, length us, event | category | flops | bytes accessed | tf_op | source)
XLA Modules:
  0.0 89.5 jit_solution(10711889089874789953)
XLA Ops:
  0.6 1.4 %copy.12.rweight = f32[128,2]{1,0:T(8,128)} copy(f32[128,2]{0,1:T(2,128)} %param.10) | data formatting | bytes 2048 | tf_op args[3]
  2.0 75.8 %routed.1 = (bf16[128,3072]{1,0:T(8,128)(2,1)}, bf16[128,3072]{1,0:T(8,128)(2,1)}, bf16[2,2,4,64,1536]{4,3,2,1,0:T(8,128)(2,1)}, bf16[3,256,1024]{2,1,0:T(8,128)(2,1)}) custom-call(bf16[128,3072]{1,0:T(8,128)(2,1)} %tokens.1, bf16[128,3072]{1,0:T(8,128)(2,1)} %cotangent.1, s32[2,128]{1,0:T(2,128)} %bitcast.12, f32[2,128]{1,0:T(2,128)} %bitcast.11, ...), custom_call_target="tpu_custom_call" | custom-call | tf_op jit(solution)/shard_map/routed/pallas_call | solution.py:338
  77.9 0.0 copy-start.1
  77.9 0.0 copy-start
  77.9 9.8 %grads.1 = (bf16[3072,1024]{1,0:T(8,128)(2,1)}, bf16[3072,1024]{1,0:T(8,128)(2,1)}, bf16[1024,3072]{1,0:T(8,128)(2,1)}) custom-call(bf16[2,2,4,64,1536]{4,3,2,1,0:T(8,128)(2,1)} %get-tuple-element.14.x.dy, bf16[2,2,4,64,1536]{4,3,2,1,0:T(8,128)(2,1)} %get-tuple-element.14.x.dy, bf16[3,256,1024]{2,1,0:T(8,128)(2,1)} %get-tuple-element.15.hid), custom_call_target="tpu_custom_call" | custom-call | tf_op jit(solution)/shard_map/grads/pallas_call | solution.py:386
  87.7 0.0 copy-done.1
  87.7 0.9 copy.15
  88.6 0.0 copy-done
  88.6 0.9 copy.16
Async XLA Ops:
  77.9 9.8 %copy-start.1 = (bf16[128,3072]{1,0:T(8,128)(2,1)S(1)}, bf16[128,3072]{1,0:T(8,128)(2,1)}, u32[]{:S(2)}) copy-start(bf16[128,3072]{1,0:T(8,128)(2,1)} %get-tuple-element.24) | copy-start | bytes 2359300
  77.9 10.7 %copy-start = (bf16[128,3072]{1,0:T(8,128)(2,1)S(1)}, bf16[128,3072]{1,0:T(8,128)(2,1)}, u32[]{:S(2)}) copy-start(bf16[128,3072]{1,0:T(8,128)(2,1)} %get-tuple-element.25) | copy-start | bytes 2359300

commit v3 on v2

--- a/solution.py
+++ b/solution.py
@@ -293,7 +293,7 @@
             sends.append(cp)
 
     todo = [
-        (i + lag * t, t, q, i) for i in range(len(stages) + 1) for t in range(2) for q in range(chunks)
+        (i + lag * t + 0.5 * q, t, q, i) for i in range(len(stages) + 1) for t in range(2) for q in range(chunks)
     ]
     for _, t, q, i in sorted(todo):
         advance(t, q, i)
@@ -336,7 +336,7 @@
     dma = pltpu.SemaphoreType.DMA
     V = pltpu.VMEM
     output, input_grad, slots, hid = pl.pallas_call(
-        functools.partial(routed_kernel, n, nz, cap, tile, chunks, 2),
+        functools.partial(routed_kernel, n, nz, cap, tile, chunks, 1),
         out_shape=(
             jax.ShapeDtypeStruct((toks, features), BF16),
             jax.ShapeDtypeStruct((toks, features), BF16),

time: 89.8 us -> 83.8 us (0.933)
  Pallas kernels: 85.6 us -> 79.6 us
    pallas_call x1, Pallas kernels: 75.8 us -> 69.8 us  [fused(): pl.pallas_call(functools.partial(routed_kernel, n, nz, cap, tile, chunks,...]
where the time goes in v3:
time: 83.8 us; the launch traced here: 83.5 us
  Pallas kernels  79.6 us (95%)
  local copies, waits for them, and re-layouts  3.18 us (4%)
    pallas_call x1, Pallas kernels, fused(): pl.pallas_call(functools.partial(routed_kernel, n, nz, cap, tile, chunks,...  69.8 us
    pallas_call x1, Pallas kernels, fused(): pl.pallas_call(grads_kernel, grid=(features // wide,), out_shape=(jax.Sha...  9.79 us
    unnamed x7, local copies, waits for them, and re-layouts  3.18 us

profile of v3, /device:TPU:0, one launch (start us, length us, event | category | flops | bytes accessed | tf_op | source)
XLA Modules:
  0.0 83.5 jit_solution(16547921801876587713)
XLA Ops:
  0.6 1.4 %copy.12.rweight = f32[128,2]{1,0:T(8,128)} copy(f32[128,2]{0,1:T(2,128)} %param.10) | data formatting | bytes 2048 | tf_op args[3]
  2.0 69.8 %routed.1 = (bf16[128,3072]{1,0:T(8,128)(2,1)}, bf16[128,3072]{1,0:T(8,128)(2,1)}, bf16[2,2,4,64,1536]{4,3,2,1,0:T(8,128)(2,1)}, bf16[3,256,1024]{2,1,0:T(8,128)(2,1)}) custom-call(bf16[128,3072]{1,0:T(8,128)(2,1)} %tokens.1, bf16[128,3072]{1,0:T(8,128)(2,1)} %cotangent.1, s32[2,128]{1,0:T(2,128)} %bitcast.12, f32[2,128]{1,0:T(2,128)} %bitcast.11, ...), custom_call_target="tpu_custom_call" | custom-call | tf_op jit(solution)/shard_map/routed/pallas_call | solution.py:338
  71.9 0.0 copy-start.1
  71.9 0.0 copy-start
  71.9 9.8 %grads.1 = (bf16[3072,1024]{1,0:T(8,128)(2,1)}, bf16[3072,1024]{1,0:T(8,128)(2,1)}, bf16[1024,3072]{1,0:T(8,128)(2,1)}) custom-call(bf16[2,2,4,64,1536]{4,3,2,1,0:T(8,128)(2,1)} %get-tuple-element.14.x.dy, bf16[2,2,4,64,1536]{4,3,2,1,0:T(8,128)(2,1)} %get-tuple-element.14.x.dy, bf16[3,256,1024]{2,1,0:T(8,128)(2,1)} %get-tuple-element.15.hid), custom_call_target="tpu_custom_call" | custom-call | tf_op jit(solution)/shard_map/grads/pallas_call | solution.py:386
  81.7 0.0 copy-done.1
  81.7 0.9 %copy.15 = bf16[128,3072]{1,0:T(8,128)(2,1)} copy(bf16[128,3072]{1,0:T(8,128)(2,1)S(1)} %copy-done.1) | data formatting | bytes 1572864
  82.6 0.0 copy-done
  82.6 0.9 %copy.16 = bf16[128,3072]{1,0:T(8,128)(2,1)} copy(bf16[128,3072]{1,0:T(8,128)(2,1)S(1)} %copy-done) | data formatting | bytes 1572864
Async XLA Ops:
  71.9 9.8 %copy-start.1 = (bf16[128,3072]{1,0:T(8,128)(2,1)S(1)}, bf16[128,3072]{1,0:T(8,128)(2,1)}, u32[]{:S(2)}) copy-start(bf16[128,3072]{1,0:T(8,128)(2,1)} %get-tuple-element.24) | copy-start | bytes 2359300
  71.9 10.7 %copy-start = (bf16[128,3072]{1,0:T(8,128)(2,1)S(1)}, bf16[128,3072]{1,0:T(8,128)(2,1)}, u32[]{:S(2)}) copy-start(bf16[128,3072]{1,0:T(8,128)(2,1)} %get-tuple-element.25) | copy-start | bytes 2359300
